TPU v7x, 32 devices: a whole 2x2x4 slice. The times are simulated.
32 devices in a mesh: row: 4 (over y, x), col: 8 (over z, core).
Axes of the slice: x: 2, y: 2, z: 4, core: 2. Of those that a mesh axis runs over, the one named last changes fastest.
Arguments:
- right_side: bfloat16 [4, 8, 8, 128, 256], P('row', 'col'), may hold values from -6 to 6
- diag_inverse: bfloat16 [4, 8, 8, 128, 128], P('row', 'col'), may hold values from -0.5 to 0.5
- panels: bfloat16 [7, 4, 400, 128, 128], P(None, 'row', 'col'), may hold values from -0.0546875 to 0.0546875
- tile_source: int32 [7, 4, 400], P(None, 'row', 'col'), may hold values from 0 to 3
- tile_target: int32 [7, 4, 400], P(None, 'row', 'col'), may hold values from 0 to 7
Outputs:
- solution: float32 [4, 8, 8, 128, 256], P('row', 'col')
All inputs are finite; a program needn't handle non-finite values.
Results may differ from a plain program's by a relative error of at most 0.017.
Values may be sent and summed in bfloat16 or wider, within the bound.
No kernel may reach another device: no remote copies, remote signals or barrier semaphores. Data moves between devices by JAX's collectives and lax.ppermute only.
A program may use at most 128 MiB of HBM per device.

v0:
```python
import jax
import jax.numpy as jnp
from jax import lax
from jax.sharding import PartitionSpec as P


def local_update(segment, panel, source, target):
    columns = lax.axis_size("col")
    picked = jnp.take(segment, source, axis=0)
    prods = jnp.einsum("qab,qbc->qac", panel, picked, preferred_element_type=jnp.float32)
    onehot = (target[None, :] == jnp.arange(columns, dtype=jnp.int32)[:, None]).astype(jnp.float32)
    sums = jnp.dot(onehot, prods.reshape(prods.shape[0], -1), precision=lax.Precision.HIGHEST)
    return sums.reshape(columns, prods.shape[1], prods.shape[2]).astype(jnp.bfloat16)


def advance_whole(block, panel, source, target):
    segment = lax.all_gather(block.astype(jnp.bfloat16)[None], "row", axis=0, tiled=True)
    partial_value = local_update(segment, panel, source, target)
    return lax.psum_scatter(partial_value, "col", scatter_dimension=0, tiled=True).astype(
        jnp.float32
    )[0]


def local(right_side, diag_inverse, panels, tile_source, tile_target):
    sections = right_side.shape[2]
    width = right_side.shape[4]
    bounds = [(0, width)]
    incoming = [None for bound in bounds]
    solved = []
    for section in range(sections):
        lower, upper = bounds[0]
        current = right_side[0, 0, section, :, lower:upper].astype(jnp.float32)
        if section > 0:
            current = current - incoming[0]
        block = jnp.dot(
            diag_inverse[0, 0, section],
            current.astype(jnp.bfloat16),
            preferred_element_type=jnp.float32,
        )
        if section + 1 < sections:
            incoming[0] = advance_whole(
                block, panels[section, 0], tile_source[section, 0], tile_target[section, 0]
            )
        solved.append(block)
    return jnp.stack(solved, axis=0)[None, None]


def solution(mesh):
    return jax.shard_map(
        local,
        mesh=mesh,
        in_specs=(
            P("row", "col", None, None, None),
            P("row", "col", None, None, None),
            P(None, "row", "col", None, None),
            P(None, "row", "col"),
            P(None, "row", "col"),
        ),
        out_specs=P("row", "col", None, None, None),
        check_vma=False,
    )
```

profile of v0, /device:TPU:0, one launch (start us, length us, event | category | flops | bytes accessed | tf_op | source)
XLA Modules:
  0.0 471.4 jit_solution(18376820517892712203)
XLA Ops:
  8.2 10.5 %all-gather = bf16[512,256]{1,0:T(8,128)(2,1)S(1)} all-gather(bf16[128,256]{1,0:T(8,128)(2,1)S(1)} %get-tuple-element.40), channel_id=2, replica_groups=mesh['row'=4,'col'=8] {'row'}, dimensions={0}, use_global_device_ids=true | all-gather | bytes 327680 | tf_op jit(solution)/shard_map/all_gather | solution.py:17
  26.1 8.2 %copy.56 = f32[50,128,256]{2,1,0:T(8,128)} copy(f32[50,128,256]{1,2,0:T(8,128)} %fusion.35) | data formatting | bytes 13107200 | tf_op jit(solution)/shard_map/qab,qbc->qac/dot_general | solution.py:10
  45.2 31.7 %reduce-scatter.8.cloned.1.call-done = bf16[1,128,256]{2,1,0:T(8,128)(2,1)} async-done(((bf16[8,128,256]{2,1,0:T(8,128)(2,1)}), bf16[1,128,256]{2,1,0:T(8,128)(2,1)}) %reduce-scatter.8.cloned.1.call-update) | async-done | bytes 65552 | tf_op jit(solution)/shard_map/reduce_scatter | solution.py:19
  78.6 9.0 %all-gather.1 = bf16[512,256]{1,0:T(8,128)(2,1)S(1)} all-gather(bf16[128,256]{1,0:T(8,128)(2,1)S(1)} %bitcast.364), channel_id=3, replica_groups=mesh['row'=4,'col'=8] {'row'}, dimensions={0}, use_global_device_ids=true | all-gather | bytes 327680 | tf_op jit(solution)/shard_map/all_gather | solution.py:17
  93.7 8.2 %copy.61 = f32[50,128,256]{2,1,0:T(8,128)} copy(f32[50,128,256]{1,2,0:T(8,128)} %fusion.38) | data formatting | bytes 13107200 | tf_op jit(solution)/shard_map/qab,qbc->qac/dot_general | solution.py:10
  105.2 6.1 %fusion.80 = bf16[8,128,256]{2,0,1:T(8,128)(2,1)S(1)} fusion(f32[128,256,50]{1,0,2:T(8,128)S(1)} %slice_bitcast_fusion.5, s32[50]{0:T(128)S(1)} %copy-done.3), kind=kOutput, calls=%fused_computation.78 | convolution fusion | flops 157548944 | bytes 7078088 | tf_op jit(solution)/shard_map/dot_general | solution.py:12
  112.3 28.8 %reduce-scatter.10.cloned.1.call-done = bf16[1,128,256]{2,1,0:T(8,128)(2,1)} async-done(((bf16[8,128,256]{2,1,0:T(8,128)(2,1)}), bf16[1,128,256]{2,1,0:T(8,128)(2,1)}) %reduce-scatter.10.cloned.1.call-update) | async-done | bytes 65552 | tf_op jit(solution)/shard_map/reduce_scatter | solution.py:19
  142.8 9.5 %all-gather.2 = bf16[512,256]{1,0:T(8,128)(2,1)S(1)} all-gather(bf16[128,256]{1,0:T(8,128)(2,1)S(1)} %bitcast.365), channel_id=4, replica_groups=mesh['row'=4,'col'=8] {'row'}, dimensions={0}, use_global_device_ids=true | all-gather | bytes 327680 | tf_op jit(solution)/shard_map/all_gather | solution.py:17
  158.3 8.2 %copy.66 = f32[50,128,256]{2,1,0:T(8,128)} copy(f32[50,128,256]{1,2,0:T(8,128)} %fusion.41) | data formatting | bytes 13107200 | tf_op jit(solution)/shard_map/qab,qbc->qac/dot_general | solution.py:10
  169.8 6.1 %fusion.83 = bf16[8,128,256]{2,0,1:T(8,128)(2,1)S(1)} fusion(f32[128,256,50]{1,0,2:T(8,128)S(1)} %slice_bitcast_fusion.4, s32[50]{0:T(128)S(1)} %copy-done.2), kind=kOutput, calls=%fused_computation.79 | convolution fusion | flops 157548944 | bytes 7078088 | tf_op jit(solution)/shard_map/dot_general | solution.py:12
  176.9 28.7 %reduce-scatter.12.cloned.1.call-done = bf16[1,128,256]{2,1,0:T(8,128)(2,1)} async-done(((bf16[8,128,256]{2,1,0:T(8,128)(2,1)}), bf16[1,128,256]{2,1,0:T(8,128)(2,1)}) %reduce-scatter.12.cloned.1.call-update) | async-done | bytes 65552 | tf_op jit(solution)/shard_map/reduce_scatter | solution.py:19
  207.4 8.9 %all-gather.3 = bf16[512,256]{1,0:T(8,128)(2,1)S(1)} all-gather(bf16[128,256]{1,0:T(8,128)(2,1)S(1)} %bitcast.366), channel_id=5, replica_groups=mesh['row'=4,'col'=8] {'row'}, dimensions={0}, use_global_device_ids=true | all-gather | bytes 327680 | tf_op jit(solution)/shard_map/all_gather | solution.py:17
  222.4 8.2 %copy.71 = f32[50,128,256]{2,1,0:T(8,128)} copy(f32[50,128,256]{1,2,0:T(8,128)} %fusion.44) | data formatting | bytes 13107200 | tf_op jit(solution)/shard_map/qab,qbc->qac/dot_general | solution.py:10
  233.9 6.1 %fusion.86 = bf16[8,128,256]{2,0,1:T(8,128)(2,1)S(1)} fusion(f32[128,256,50]{1,0,2:T(8,128)S(1)} %slice_bitcast_fusion.3, s32[50]{0:T(128)S(1)} %copy-done.1), kind=kOutput, calls=%fused_computation.80 | convolution fusion | flops 157548944 | bytes 7078088 | tf_op jit(solution)/shard_map/dot_general | solution.py:12
  241.0 28.8 %reduce-scatter.14.cloned.1.call-done = bf16[1,128,256]{2,1,0:T(8,128)(2,1)} async-done(((bf16[8,128,256]{2,1,0:T(8,128)(2,1)}), bf16[1,128,256]{2,1,0:T(8,128)(2,1)}) %reduce-scatter.14.cloned.1.call-update) | async-done | bytes 65552 | tf_op jit(solution)/shard_map/reduce_scatter | solution.py:19
  271.5 9.3 %all-gather.4 = bf16[512,256]{1,0:T(8,128)(2,1)S(1)} all-gather(bf16[128,256]{1,0:T(8,128)(2,1)S(1)} %bitcast.367), channel_id=6, replica_groups=mesh['row'=4,'col'=8] {'row'}, dimensions={0}, use_global_device_ids=true | all-gather | bytes 327680 | tf_op jit(solution)/shard_map/all_gather | solution.py:17
  286.8 8.2 %copy.76 = f32[50,128,256]{2,1,0:T(8,128)} copy(f32[50,128,256]{1,2,0:T(8,128)} %fusion.47) | data formatting | bytes 13107200 | tf_op jit(solution)/shard_map/qab,qbc->qac/dot_general | solution.py:10
  305.5 28.5 %reduce-scatter.16.cloned.1.call-done = bf16[1,128,256]{2,1,0:T(8,128)(2,1)} async-done(((bf16[8,128,256]{2,1,0:T(8,128)(2,1)}), bf16[1,128,256]{2,1,0:T(8,128)(2,1)}) %reduce-scatter.16.cloned.1.call-update) | async-done | bytes 65552 | tf_op jit(solution)/shard_map/reduce_scatter | solution.py:19
  335.6 9.2 %all-gather.5 = bf16[512,256]{1,0:T(8,128)(2,1)S(1)} all-gather(bf16[128,256]{1,0:T(8,128)(2,1)S(1)} %bitcast.368), channel_id=7, replica_groups=mesh['row'=4,'col'=8] {'row'}, dimensions={0}, use_global_device_ids=true | all-gather | bytes 327680 | tf_op jit(solution)/shard_map/all_gather | solution.py:17
  350.9 8.2 %copy.81 = f32[50,128,256]{2,1,0:T(8,128)} copy(f32[50,128,256]{1,2,0:T(8,128)} %fusion.50) | data formatting | bytes 13107200 | tf_op jit(solution)/shard_map/qab,qbc->qac/dot_general | solution.py:10
  369.5 28.6 %reduce-scatter.18.cloned.1.call-done = bf16[1,128,256]{2,1,0:T(8,128)(2,1)} async-done(((bf16[8,128,256]{2,1,0:T(8,128)(2,1)}), bf16[1,128,256]{2,1,0:T(8,128)(2,1)}) %reduce-scatter.18.cloned.1.call-update) | async-done | bytes 65552 | tf_op jit(solution)/shard_map/reduce_scatter | solution.py:19
  399.8 9.7 %all-gather.6 = bf16[512,256]{1,0:T(8,128)(2,1)S(1)} all-gather(bf16[128,256]{1,0:T(8,128)(2,1)S(1)} %bitcast.369), channel_id=8, replica_groups=mesh['row'=4,'col'=8] {'row'}, dimensions={0}, use_global_device_ids=true | all-gather | bytes 327680 | tf_op jit(solution)/shard_map/all_gather | solution.py:17
  415.6 8.2 %copy.86 = f32[50,128,256]{2,1,0:T(8,128)} copy(f32[50,128,256]{1,2,0:T(8,128)} %fusion.53) | data formatting | bytes 13107200 | tf_op jit(solution)/shard_map/qab,qbc->qac/dot_general | solution.py:10
  434.1 28.7 %reduce-scatter.20.cloned.1.call-done = bf16[1,128,256]{2,1,0:T(8,128)(2,1)} async-done(((bf16[8,128,256]{2,1,0:T(8,128)(2,1)}), bf16[1,128,256]{2,1,0:T(8,128)(2,1)}) %reduce-scatter.20.cloned.1.call-update) | async-done | bytes 65552 | tf_op jit(solution)/shard_map/reduce_scatter | solution.py:19
  (87 shorter events, 112.0 us)
Async XLA Ops:
  6.5 70.4 %reduce-scatter.8.cloned.1.call-start = ((), (), s32[]{:S(2)}) async-start(), calls=%async_computation.7 | async-start | bytes 589824 | tf_op jit(solution)/shard_map/reduce_scatter | solution.py:19
  34.3 3.3 copy-start
  37.6 7.6 %copy-start.11 = (s32[50]{0:T(128)S(1)}, s32[50]{0:T(128)}, u32[]{:S(2)}) copy-start(s32[50]{0:T(128)} %get-tuple-element.34) | copy-start | bytes 604
  45.2 95.9 %reduce-scatter.10.cloned.1.call-start = ((), (), s32[]{:S(2)}) async-start(), calls=%async_computation.8 | async-start | bytes 589824 | tf_op jit(solution)/shard_map/reduce_scatter | solution.py:19
  101.9 3.3 copy-start.3
  105.2 7.1 %copy-start.10 = (s32[50]{0:T(128)S(1)}, s32[50]{0:T(128)}, u32[]{:S(2)}) copy-start(s32[50]{0:T(128)} %get-tuple-element.32) | copy-start | bytes 604
  112.3 93.4 %reduce-scatter.12.cloned.1.call-start = ((), (), s32[]{:S(2)}) async-start(), calls=%async_computation.9 | async-start | bytes 589824 | tf_op jit(solution)/shard_map/reduce_scatter | solution.py:19
  166.5 3.3 copy-start.2
  169.8 7.1 %copy-start.9 = (s32[50]{0:T(128)S(1)}, s32[50]{0:T(128)}, u32[]{:S(2)}) copy-start(s32[50]{0:T(128)} %get-tuple-element.30) | copy-start | bytes 604
  176.9 92.9 %reduce-scatter.14.cloned.1.call-start = ((), (), s32[]{:S(2)}) async-start(), calls=%async_computation.10 | async-start | bytes 589824 | tf_op jit(solution)/shard_map/reduce_scatter | solution.py:19
  230.6 3.3 copy-start.1
  233.9 7.1 %copy-start.8 = (s32[50]{0:T(128)S(1)}, s32[50]{0:T(128)}, u32[]{:S(2)}) copy-start(s32[50]{0:T(128)} %get-tuple-element.28) | copy-start | bytes 604
  240.9 93.0 %reduce-scatter.16.cloned.1.call-start = ((), (), s32[]{:S(2)}) async-start(), calls=%async_computation.11 | async-start | bytes 589824 | tf_op jit(solution)/shard_map/reduce_scatter | solution.py:19
  298.3 7.1 %copy-start.7 = (s32[50]{0:T(128)S(1)}, s32[50]{0:T(128)}, u32[]{:S(2)}) copy-start(s32[50]{0:T(128)} %get-tuple-element.38) | copy-start | bytes 604
  304.4 41.2 %copy-start.5 = (pred[50]{0:T(512)(128)(4,1)S(1)}, pred[50]{0:T(512)(128)(4,1)}, u32[]{:S(2)}) copy-start(pred[50]{0:T(512)(128)(4,1)} %get-tuple-element.37) | copy-start | bytes 154
  305.4 92.7 %reduce-scatter.18.cloned.1.call-start = ((), (), s32[]{:S(2)}) async-start(), calls=%async_computation.12 | async-start | bytes 589824 | tf_op jit(solution)/shard_map/reduce_scatter | solution.py:19
  362.4 7.1 %copy-start.6 = (s32[50]{0:T(128)S(1)}, s32[50]{0:T(128)}, u32[]{:S(2)}) copy-start(s32[50]{0:T(128)} %get-tuple-element.7) | copy-start | bytes 604
  362.4 47.8 %copy-start.4 = (pred[50]{0:T(512)(128)(4,1)S(1)}, pred[50]{0:T(512)(128)(4,1)}, u32[]{:S(2)}) copy-start(pred[50]{0:T(512)(128)(4,1)} %get-tuple-element.6) | copy-start | bytes 154
  369.5 93.3 %reduce-scatter.20.cloned.1.call-start = ((), (), s32[]{:S(2)}) async-start(), calls=%async_computation.13 | async-start | bytes 589824 | tf_op jit(solution)/shard_map/reduce_scatter | solution.py:19
Sparse Core Ops, SparseCore 0:
  45.3 31.5 reduce-scatter.7
  112.4 28.6 reduce-scatter.9
  177.0 28.6 reduce-scatter.11
  241.1 28.6 reduce-scatter.13
  305.5 28.3 reduce-scatter.15
  369.6 28.4 reduce-scatter.17
  434.2 28.5 reduce-scatter.19
where the time goes:
time: 480 us; the launch traced here: 471 us
  waiting for transfers between devices  204 us (42%)
  matrix products  93.2 us (19%)
  local copies, waits for them, and re-layouts  92.6 us (19%)
  blocking collectives  66.1 us (14%)
  between operations  14 us (3%)
    reduce_scatter x7, waiting for transfers between devices, advance_whole(): lax.psum_scatter(partial_value, 'col', scatter_dimension=0, tiled=True)  204 us
    all_gather x7, blocking collectives, advance_whole(): lax.all_gather(block.astype(jnp.bfloat16)[None], 'row', axis=0, tiled=True)  66.1 us
    dot_general x7, local copies, waits for them, and re-layouts, local_update(): jnp.einsum('qab,qbc->qac', panel, picked, preferred_element_type=jnp.floa...  57.4 us
    dot_general x7, matrix products, local_update(): jnp.dot(onehot, prods.reshape(prods.shape[0], -1), precision=lax.Precisio...  42.7 us
    dot_general x7, matrix products, local_update(): jnp.einsum('qab,qbc->qac', panel, picked, preferred_element_type=jnp.floa...  37 us
    dot_general x7, local copies, waits for them, and re-layouts, local_update(): jnp.dot(onehot, prods.reshape(prods.shape[0], -1), precision=lax.Precisio...  23 us
    dot_general x8, matrix products, local(): jnp.dot(diag_inverse[0, 0, section], current.astype(jnp.bfloat16), prefer...  13.5 us
  transfers between devices with their start and end apart: 7, of which 7 were waited for; matrix products, arithmetic and copies ran while one was open for 0% of the time, Pallas kernels for 0%

commit v1 on v0

--- a/solution.py
+++ b/solution.py
@@ -2,6 +2,11 @@
 import jax.numpy as jnp
 from jax import lax
 from jax.sharding import PartitionSpec as P
+
+
+def gather_from_all(x, axis, dim):
+    copies = jnp.concatenate([x] * lax.axis_size(axis), axis=dim)
+    return lax.all_to_all(copies, axis, dim, dim, tiled=True)
 
 
 def local_update(segment, panel, source, target):
@@ -14,7 +19,7 @@
 
 
 def advance_whole(block, panel, source, target):
-    segment = lax.all_gather(block.astype(jnp.bfloat16)[None], "row", axis=0, tiled=True)
+    segment = gather_from_all(block.astype(jnp.bfloat16)[None], "row", 0)
     partial_value = local_update(segment, panel, source, target)
     return lax.psum_scatter(partial_value, "col", scatter_dimension=0, tiled=True).astype(
         jnp.float32

time: 480 us -> 484 us (level)
  blocking collectives: 66.1 us -> 0 us
  waiting for transfers between devices: 204 us -> 238 us
  starting transfers between devices: 0.25 us -> 28.8 us
  local copies, waits for them, and re-layouts: 92.6 us -> 98.2 us
    all_gather x7 -> x0, blocking collectives: 66.1 us -> none  [advance_whole(): lax.all_gather(block.astype(jnp.bfloat16)[None], 'row', axis=0, tiled=True)]
    all_to_all x0 -> x7, waiting for transfers between devices: none -> 33.1 us  [gather_from_all(): return lax.all_to_all(copies, axis, dim, dim, tiled=True)]
    all_to_all x0 -> x7, starting transfers between devices: none -> 27.2 us  [gather_from_all(): return lax.all_to_all(copies, axis, dim, dim, tiled=True)]
    concatenate x0 -> x7, local copies, waits for them, and re-layouts: none -> 4.96 us  [gather_from_all(): copies = jnp.concatenate([x] * lax.axis_size(axis), axis=dim)]
  transfers between devices with their start and end apart: 7 -> 14, of which waited for: 7 -> 14; matrix products, arithmetic and copies ran while one was open for 0% -> 1% of each run, Pallas kernels for 0% -> 0%
where the time goes in v1:
time: 484 us; the launch traced here: 475 us
  waiting for transfers between devices  238 us (49%)
  local copies, waits for them, and re-layouts  98.2 us (20%)
  matrix products  93.6 us (19%)
  starting transfers between devices  28.8 us (6%)
  between operations  14.3 us (3%)
    reduce_scatter x7, waiting for transfers between devices, advance_whole(): lax.psum_scatter(partial_value, 'col', scatter_dimension=0, tiled=True)  205 us
    dot_general x7, local copies, waits for them, and re-layouts, local_update(): jnp.einsum('qab,qbc->qac', panel, picked, preferred_element_type=jnp.floa...  57.4 us
    dot_general x7, matrix products, local_update(): jnp.dot(onehot, prods.reshape(prods.shape[0], -1), precision=lax.Precisio...  42.7 us
    dot_general x7, matrix products, local_update(): jnp.einsum('qab,qbc->qac', panel, picked, preferred_element_type=jnp.floa...  37.3 us
    all_to_all x7, waiting for transfers between devices, gather_from_all(): return lax.all_to_all(copies, axis, dim, dim, tiled=True)  33.1 us
    all_to_all x7, starting transfers between devices, gather_from_all(): return lax.all_to_all(copies, axis, dim, dim, tiled=True)  27.2 us
    dot_general x7, local copies, waits for them, and re-layouts, local_update(): jnp.dot(onehot, prods.reshape(prods.shape[0], -1), precision=lax.Precisio...  23 us
    dot_general x8, matrix products, local(): jnp.dot(diag_inverse[0, 0, section], current.astype(jnp.bfloat16), prefer...  13.5 us
  transfers between devices with their start and end apart: 14, of which 14 were waited for; matrix products, arithmetic and copies ran while one was open for 1% of the time, Pallas kernels for 0%

profile of v1, /device:TPU:0, one launch (start us, length us, event | category | flops | bytes accessed | tf_op | source)
XLA Modules:
  0.0 474.6 jit_solution(8009915956248128005)
XLA Ops:
  25.6 8.2 %copy.56 = f32[50,128,256]{2,1,0:T(8,128)} copy(f32[50,128,256]{1,2,0:T(8,128)} %fusion.35) | data formatting | bytes 13107200 | tf_op jit(solution)/shard_map/qab,qbc->qac/dot_general | solution.py:15
  37.1 6.1 %fusion.77 = bf16[8,128,256]{2,0,1:T(8,128)(2,1)S(1)} fusion(f32[128,256,50]{1,0,2:T(8,128)S(1)} %slice_bitcast_fusion.6, s32[50]{0:T(128)S(1)} %copy-done.3), kind=kOutput, calls=%fused_computation.77 | convolution fusion | flops 157548944 | bytes 7078088 | tf_op jit(solution)/shard_map/dot_general | solution.py:17
  44.1 31.5 %reduce-scatter.8.cloned.1.call-done = bf16[1,128,256]{2,1,0:T(8,128)(2,1)} async-done(((bf16[8,128,256]{2,1,0:T(8,128)(2,1)}), bf16[1,128,256]{2,1,0:T(8,128)(2,1)}) %reduce-scatter.8.cloned.1.call-update) | async-done | bytes 65552 | tf_op jit(solution)/shard_map/reduce_scatter | solution.py:24
  87.9 5.3 %fusion.38 = f32[50,128,256]{1,2,0:T(8,128)} fusion(bf16[50,128,256]{2,1,0:T(8,128)(2,1)S(1)} %gather_fusion.1, pred[50]{0:T(512)(128)(4,1)} %get-tuple-element.33, bf16[7,1,50,128,128]{4,3,2,1,0:T(8,128)(2,1)} %param.9), kind=kOutput, calls=%fused_computation.50 | convolution fusion | flops 421068800 | bytes 11469312 | tf_op jit(solution)/shard_map/qab,qbc->qac/dot_general | solution.py:15
  93.2 8.2 %copy.61 = f32[50,128,256]{2,1,0:T(8,128)} copy(f32[50,128,256]{1,2,0:T(8,128)} %fusion.38) | data formatting | bytes 13107200 | tf_op jit(solution)/shard_map/qab,qbc->qac/dot_general | solution.py:15
  104.7 6.1 %fusion.80 = bf16[8,128,256]{2,0,1:T(8,128)(2,1)S(1)} fusion(f32[128,256,50]{1,0,2:T(8,128)S(1)} %slice_bitcast_fusion.5, s32[50]{0:T(128)S(1)} %copy-done.2), kind=kOutput, calls=%fused_computation.78 | convolution fusion | flops 157548944 | bytes 7078088 | tf_op jit(solution)/shard_map/dot_general | solution.py:17
  111.7 28.9 %reduce-scatter.10.cloned.1.call-done = bf16[1,128,256]{2,1,0:T(8,128)(2,1)} async-done(((bf16[8,128,256]{2,1,0:T(8,128)(2,1)}), bf16[1,128,256]{2,1,0:T(8,128)(2,1)}) %reduce-scatter.10.cloned.1.call-update) | async-done | bytes 65552 | tf_op jit(solution)/shard_map/reduce_scatter | solution.py:24
  152.9 5.3 %fusion.41 = f32[50,128,256]{1,2,0:T(8,128)} fusion(bf16[50,128,256]{2,1,0:T(8,128)(2,1)S(1)} %gather_fusion.2, pred[50]{0:T(512)(128)(4,1)} %get-tuple-element.31, bf16[7,1,50,128,128]{4,3,2,1,0:T(8,128)(2,1)} %param.9), kind=kOutput, calls=%fused_computation.51 | convolution fusion | flops 421068800 | bytes 11469312 | tf_op jit(solution)/shard_map/qab,qbc->qac/dot_general | solution.py:15
  158.2 8.2 %copy.66 = f32[50,128,256]{2,1,0:T(8,128)} copy(f32[50,128,256]{1,2,0:T(8,128)} %fusion.41) | data formatting | bytes 13107200 | tf_op jit(solution)/shard_map/qab,qbc->qac/dot_general | solution.py:15
  169.8 6.1 %fusion.83 = bf16[8,128,256]{2,0,1:T(8,128)(2,1)S(1)} fusion(f32[128,256,50]{1,0,2:T(8,128)S(1)} %slice_bitcast_fusion.4, s32[50]{0:T(128)S(1)} %copy-done.1), kind=kOutput, calls=%fused_computation.79 | convolution fusion | flops 157548944 | bytes 7078088 | tf_op jit(solution)/shard_map/dot_general | solution.py:17
  176.8 28.9 %reduce-scatter.12.cloned.1.call-done = bf16[1,128,256]{2,1,0:T(8,128)(2,1)} async-done(((bf16[8,128,256]{2,1,0:T(8,128)(2,1)}), bf16[1,128,256]{2,1,0:T(8,128)(2,1)}) %reduce-scatter.12.cloned.1.call-update) | async-done | bytes 65552 | tf_op jit(solution)/shard_map/reduce_scatter | solution.py:24
  223.1 8.2 %copy.71 = f32[50,128,256]{2,1,0:T(8,128)} copy(f32[50,128,256]{1,2,0:T(8,128)} %fusion.44) | data formatting | bytes 13107200 | tf_op jit(solution)/shard_map/qab,qbc->qac/dot_general | solution.py:15
  234.6 6.1 %fusion.86 = bf16[8,128,256]{2,0,1:T(8,128)(2,1)S(1)} fusion(f32[128,256,50]{1,0,2:T(8,128)S(1)} %slice_bitcast_fusion.3, s32[50]{0:T(128)S(1)} %copy-done), kind=kOutput, calls=%fused_computation.80 | convolution fusion | flops 157548944 | bytes 7078088 | tf_op jit(solution)/shard_map/dot_general | solution.py:17
  241.6 29.1 %reduce-scatter.14.cloned.1.call-done = bf16[1,128,256]{2,1,0:T(8,128)(2,1)} async-done(((bf16[8,128,256]{2,1,0:T(8,128)(2,1)}), bf16[1,128,256]{2,1,0:T(8,128)(2,1)}) %reduce-scatter.14.cloned.1.call-update) | async-done | bytes 65552 | tf_op jit(solution)/shard_map/reduce_scatter | solution.py:24
  282.8 5.3 %fusion.47 = f32[50,128,256]{1,2,0:T(8,128)} fusion(bf16[50,128,256]{2,1,0:T(8,128)(2,1)S(1)} %gather_fusion.4, pred[50]{0:T(512)(128)(4,1)} %get-tuple-element.27, bf16[7,1,50,128,128]{4,3,2,1,0:T(8,128)(2,1)} %param.9), kind=kOutput, calls=%fused_computation.53 | convolution fusion | flops 421068800 | bytes 11469312 | tf_op jit(solution)/shard_map/qab,qbc->qac/dot_general | solution.py:15
  288.1 8.2 %copy.76 = f32[50,128,256]{2,1,0:T(8,128)} copy(f32[50,128,256]{1,2,0:T(8,128)} %fusion.47) | data formatting | bytes 13107200 | tf_op jit(solution)/shard_map/qab,qbc->qac/dot_general | solution.py:15
  299.6 6.1 %fusion.89 = bf16[8,128,256]{2,0,1:T(8,128)(2,1)S(1)} fusion(f32[128,256,50]{1,0,2:T(8,128)S(1)} %slice_bitcast_fusion.2, s32[50]{0:T(128)S(1)} %get-tuple-element.21), kind=kOutput, calls=%fused_computation.81 | convolution fusion | flops 157548944 | bytes 7078088 | tf_op jit(solution)/shard_map/dot_general | solution.py:17
  306.7 29.0 %reduce-scatter.16.cloned.1.call-done = bf16[1,128,256]{2,1,0:T(8,128)(2,1)} async-done(((bf16[8,128,256]{2,1,0:T(8,128)(2,1)}), bf16[1,128,256]{2,1,0:T(8,128)(2,1)}) %reduce-scatter.16.cloned.1.call-update) | async-done | bytes 65552 | tf_op jit(solution)/shard_map/reduce_scatter | solution.py:24
  353.2 8.2 %copy.81 = f32[50,128,256]{2,1,0:T(8,128)} copy(f32[50,128,256]{1,2,0:T(8,128)} %fusion.50) | data formatting | bytes 13107200 | tf_op jit(solution)/shard_map/qab,qbc->qac/dot_general | solution.py:15
  364.7 6.1 %fusion.92 = bf16[8,128,256]{2,0,1:T(8,128)(2,1)S(1)} fusion(f32[128,256,50]{1,0,2:T(8,128)S(1)} %slice_bitcast_fusion.1, s32[50]{0:T(128)S(1)} %get-tuple-element.26), kind=kOutput, calls=%fused_computation.82 | convolution fusion | flops 157548944 | bytes 7078088 | tf_op jit(solution)/shard_map/dot_general | solution.py:17
  371.8 28.9 %reduce-scatter.18.cloned.1.call-done = bf16[1,128,256]{2,1,0:T(8,128)(2,1)} async-done(((bf16[8,128,256]{2,1,0:T(8,128)(2,1)}), bf16[1,128,256]{2,1,0:T(8,128)(2,1)}) %reduce-scatter.18.cloned.1.call-update) | async-done | bytes 65552 | tf_op jit(solution)/shard_map/reduce_scatter | solution.py:24
  418.3 8.2 %copy.86 = f32[50,128,256]{2,1,0:T(8,128)} copy(f32[50,128,256]{1,2,0:T(8,128)} %fusion.53) | data formatting | bytes 13107200 | tf_op jit(solution)/shard_map/qab,qbc->qac/dot_general | solution.py:15
  429.8 6.1 %fusion.95 = bf16[8,128,256]{2,0,1:T(8,128)(2,1)S(1)} fusion(f32[128,256,50]{1,0,2:T(8,128)S(1)} %slice_bitcast_fusion, s32[50]{0:T(128)S(1)} %get-tuple-element.20), kind=kOutput, calls=%fused_computation.83 | convolution fusion | flops 157548944 | bytes 7078088 | tf_op jit(solution)/shard_map/dot_general | solution.py:17
  436.8 28.8 %reduce-scatter.20.cloned.1.call-done = bf16[1,128,256]{2,1,0:T(8,128)(2,1)} async-done(((bf16[8,128,256]{2,1,0:T(8,128)(2,1)}), bf16[1,128,256]{2,1,0:T(8,128)(2,1)}) %reduce-scatter.20.cloned.1.call-update) | async-done | bytes 65552 | tf_op jit(solution)/shard_map/reduce_scatter | solution.py:24
  (101 shorter events, 139.1 us)
Async XLA Ops:
  8.9 10.6 %all-to-all-start = ((bf16[4,128,256]{2,1,0:T(8,128)(2,1)}), bf16[4,128,256]{2,1,0:T(8,128)(2,1)S(1)}, u32[]{:S(2)}, u32[]{:S(2)}) async-start(bf16[4,128,256]{2,1,0:T(8,128)(2,1)} %concatenate.21), calls=%async_computation | async-start | bytes 524288 | tf_op jit(solution)/shard_map/all_to_all | solution.py:9
  14.1 61.5 %reduce-scatter.8.cloned.1.call-start = ((), (), s32[]{:S(2)}) async-start(), calls=%async_computation.14 | async-start | bytes 589824 | tf_op jit(solution)/shard_map/reduce_scatter | solution.py:24
  33.8 3.3 copy-start.3
  37.1 44.9 %copy-start.11 = (s32[50]{0:T(128)S(1)}, s32[50]{0:T(128)}, u32[]{:S(2)}) copy-start(s32[50]{0:T(128)} %get-tuple-element.34) | copy-start | bytes 604
  78.0 9.1 %all-to-all-start.1 = ((bf16[4,128,256]{2,1,0:T(8,128)(2,1)}), bf16[4,128,256]{2,1,0:T(8,128)(2,1)S(1)}, u32[]{:S(2)}, u32[]{:S(2)}) async-start(bf16[4,128,256]{2,1,0:T(8,128)(2,1)} %concatenate.22), calls=%async_computation.2 | async-start | bytes 524288 | tf_op jit(solution)/shard_map/all_to_all | solution.py:9
  81.8 58.8 %reduce-scatter.10.cloned.1.call-start = ((), (), s32[]{:S(2)}) async-start(), calls=%async_computation.15 | async-start | bytes 589824 | tf_op jit(solution)/shard_map/reduce_scatter | solution.py:24
  104.7 42.5 %copy-start.10 = (s32[50]{0:T(128)S(1)}, s32[50]{0:T(128)}, u32[]{:S(2)}) copy-start(s32[50]{0:T(128)} %get-tuple-element.32) | copy-start | bytes 604
  143.0 9.1 %all-to-all-start.2 = ((bf16[4,128,256]{2,1,0:T(8,128)(2,1)}), bf16[4,128,256]{2,1,0:T(8,128)(2,1)S(1)}, u32[]{:S(2)}, u32[]{:S(2)}) async-start(bf16[4,128,256]{2,1,0:T(8,128)(2,1)} %concatenate.23), calls=%async_computation.4 | async-start | bytes 524288 | tf_op jit(solution)/shard_map/all_to_all | solution.py:9
  146.8 58.8 %reduce-scatter.12.cloned.1.call-start = ((), (), s32[]{:S(2)}) async-start(), calls=%async_computation.16 | async-start | bytes 589824 | tf_op jit(solution)/shard_map/reduce_scatter | solution.py:24
  166.4 3.3 copy-start.1
  169.7 42.1 %copy-start.9 = (s32[50]{0:T(128)S(1)}, s32[50]{0:T(128)}, u32[]{:S(2)}) copy-start(s32[50]{0:T(128)} %get-tuple-element.30) | copy-start | bytes 604
  208.0 9.0 %all-to-all-start.3 = ((bf16[4,128,256]{2,1,0:T(8,128)(2,1)}), bf16[4,128,256]{2,1,0:T(8,128)(2,1)S(1)}, u32[]{:S(2)}, u32[]{:S(2)}) async-start(bf16[4,128,256]{2,1,0:T(8,128)(2,1)} %concatenate.24), calls=%async_computation.6 | async-start | bytes 524288 | tf_op jit(solution)/shard_map/all_to_all | solution.py:9
  211.6 59.1 %reduce-scatter.14.cloned.1.call-start = ((), (), s32[]{:S(2)}) async-start(), calls=%async_computation.17 | async-start | bytes 589824 | tf_op jit(solution)/shard_map/reduce_scatter | solution.py:24
  234.6 42.3 %copy-start.8 = (s32[50]{0:T(128)S(1)}, s32[50]{0:T(128)}, u32[]{:S(2)}) copy-start(s32[50]{0:T(128)} %get-tuple-element.28) | copy-start | bytes 604
  273.1 8.9 %all-to-all-start.4 = ((bf16[4,128,256]{2,1,0:T(8,128)(2,1)}), bf16[4,128,256]{2,1,0:T(8,128)(2,1)S(1)}, u32[]{:S(2)}, u32[]{:S(2)}) async-start(bf16[4,128,256]{2,1,0:T(8,128)(2,1)} %concatenate.25), calls=%async_computation.8 | async-start | bytes 524288 | tf_op jit(solution)/shard_map/all_to_all | solution.py:9
  276.7 59.0 %reduce-scatter.16.cloned.1.call-start = ((), (), s32[]{:S(2)}) async-start(), calls=%async_computation.18 | async-start | bytes 589824 | tf_op jit(solution)/shard_map/reduce_scatter | solution.py:24
  299.6 42.4 %copy-start.7 = (s32[50]{0:T(128)S(1)}, s32[50]{0:T(128)}, u32[]{:S(2)}) copy-start(s32[50]{0:T(128)} %get-tuple-element.38) | copy-start | bytes 604
  305.7 42.2 %copy-start.5 = (pred[50]{0:T(512)(128)(4,1)S(1)}, pred[50]{0:T(512)(128)(4,1)}, u32[]{:S(2)}) copy-start(pred[50]{0:T(512)(128)(4,1)} %get-tuple-element.37) | copy-start | bytes 154
  338.1 9.0 %all-to-all-start.5 = ((bf16[4,128,256]{2,1,0:T(8,128)(2,1)}), bf16[4,128,256]{2,1,0:T(8,128)(2,1)S(1)}, u32[]{:S(2)}, u32[]{:S(2)}) async-start(bf16[4,128,256]{2,1,0:T(8,128)(2,1)} %concatenate.26), calls=%async_computation.10 | async-start | bytes 524288 | tf_op jit(solution)/shard_map/all_to_all | solution.py:9
  341.8 58.9 %reduce-scatter.18.cloned.1.call-start = ((), (), s32[]{:S(2)}) async-start(), calls=%async_computation.19 | async-start | bytes 589824 | tf_op jit(solution)/shard_map/reduce_scatter | solution.py:24
  364.7 42.4 %copy-start.6 = (s32[50]{0:T(128)S(1)}, s32[50]{0:T(128)}, u32[]{:S(2)}) copy-start(s32[50]{0:T(128)} %get-tuple-element.7) | copy-start | bytes 604
  370.8 42.1 %copy-start.4 = (pred[50]{0:T(512)(128)(4,1)S(1)}, pred[50]{0:T(512)(128)(4,1)}, u32[]{:S(2)}) copy-start(pred[50]{0:T(512)(128)(4,1)} %get-tuple-element.6) | copy-start | bytes 154
  403.1 9.1 %all-to-all-start.6 = ((bf16[4,128,256]{2,1,0:T(8,128)(2,1)}), bf16[4,128,256]{2,1,0:T(8,128)(2,1)S(1)}, u32[]{:S(2)}, u32[]{:S(2)}) async-start(bf16[4,128,256]{2,1,0:T(8,128)(2,1)} %concatenate.27), calls=%async_computation.12 | async-start | bytes 524288 | tf_op jit(solution)/shard_map/all_to_all | solution.py:9
  406.8 58.7 %reduce-scatter.20.cloned.1.call-start = ((), (), s32[]{:S(2)}) async-start(), calls=%async_computation.20 | async-start | bytes 589824 | tf_op jit(solution)/shard_map/reduce_scatter | solution.py:24
  (2 other events, 6.6 us)
Sparse Core Ops, SparseCore 0:
  44.2 31.3 reduce-scatter.7
  111.9 28.6 reduce-scatter.9
  176.9 28.6 reduce-scatter.11
  241.8 28.9 reduce-scatter.13
  306.8 28.8 reduce-scatter.15
  371.9 28.7 reduce-scatter.17
  436.9 28.6 reduce-scatter.19
